TPU v7x, 32 devices: a whole 2x2x4 slice. The times are simulated.
32 devices in a mesh: dp: 8 (over y, x, core), tensor: 4 (over z).
Axes of the slice: x: 2, y: 2, z: 4, core: 2. Of those that a mesh axis runs over, the one named last changes fastest.
Arguments:
- layer_input: bfloat16 [16384, 4096], P('dp', 'tensor'), may hold values from -54 to 54
- queries: bfloat16 [16384, 2048], P('dp', 'tensor'), may hold values from -6 to 6
- keys_values: bfloat16 [16384, 2, 1024], P('dp', None, 'tensor'), may hold values from -6 to 6
- out_grads: bfloat16 [16384, 2048], P('dp', 'tensor'), may hold values from -6 to 6
- log_sums: bfloat16 [16384, 16], P('dp', 'tensor'), may hold values from 2.5 to 5.5
- deltas: bfloat16 [16384, 16], P('dp', 'tensor'), may hold values from -1.5 to 1.5
- tile_fill: int32 [8, 16], replicated, may hold values from 1 to 128, as said below
- tile_cont: int32 [8, 16], replicated, may hold values from 0 to 1, as said below
- moment_first: float32 [4096, 2, 1024], P(('tensor', 'dp')), may hold values from -2 to 2
- moment_second: float32 [2, 8], replicated, may hold values from 0.05 to 0.5
Outputs:
- update: float32 [4096, 2, 1024], P(('tensor', 'dp'))
- new_first: float32 [4096, 2, 1024], P(('tensor', 'dp'))
- new_second: float32 [2, 8], replicated
Inputs may be any that keep to these rules, and one draw needn't show every extreme that they name: `tile_fill`: a tile followed by a tile with tile_cont 1 has all 128 positions live. Documents span one or two tiles: tile_cont is 0 for the first tile of each group and never 1 for two tiles in a row.
All inputs are finite; a program needn't handle non-finite values.
Results may differ from a plain program's by a relative error of at most 0.0055.
Values may be sent and summed in bfloat16 or wider, within the bound.
A program may use at most 64 MiB of HBM per device.

v0:
```python
import math
import jax
import jax.numpy as jnp
from jax import lax
from jax.sharding import PartitionSpec as P

D = 4096
HD = 128
ADAM_ONE = 0.9
ADAM_TWO = 0.95
ADAM_EPS = 1e-08


def band_grads(q_tiles, k_tiles, v_tiles, do_tiles, lse_tiles, delta_tiles, fill_tiles, cont_tiles):
    tile_total, block_len, groups, head_width = q_tiles.shape
    scale_qk = head_width ** (-0.5)
    zero_tile = jnp.zeros_like(k_tiles[:1])
    k_window = jnp.concatenate([jnp.concatenate([zero_tile, k_tiles[:-1]], 0), k_tiles], 1)
    v_window = jnp.concatenate([jnp.concatenate([zero_tile, v_tiles[:-1]], 0), v_tiles], 1)
    places = jnp.arange(block_len)
    live_rows = places[None, :] < fill_tiles[:, None]
    causal = places[:, None] >= places[None, :]
    own_part = live_rows[:, :, None] & causal[None]
    prev_part = (
        live_rows[:, :, None] & (cont_tiles[:, None, None] == 1) & (places[None, None, :] >= 0)
    )
    allowed = jnp.concatenate([prev_part, own_part], 2)[:, None]
    scores = (
        jnp.einsum("sqgd,skd->sgqk", q_tiles, k_window, preferred_element_type=jnp.float32)
        * scale_qk
    )
    lse_rows = jnp.swapaxes(lse_tiles.astype(jnp.float32), 1, 2)[..., None]
    delta_rows = jnp.swapaxes(delta_tiles.astype(jnp.float32), 1, 2)[..., None]
    prob_vals = jnp.where(allowed, jnp.exp(scores - lse_rows), 0.0)
    dprobs = jnp.einsum("sqgd,skd->sgqk", do_tiles, v_window, preferred_element_type=jnp.float32)
    dscores = prob_vals * (dprobs - delta_rows)
    value_grad = jnp.einsum(
        "sgqk,sqgd->skd",
        prob_vals.astype(jnp.bfloat16),
        do_tiles,
        preferred_element_type=jnp.float32,
    )
    key_grad = (
        jnp.einsum(
            "sgqk,sqgd->skd",
            dscores.astype(jnp.bfloat16),
            q_tiles,
            preferred_element_type=jnp.float32,
        )
        * scale_qk
    )
    key_out = key_grad[:, block_len:] + jnp.concatenate(
        [key_grad[1:, :block_len], jnp.zeros_like(key_grad[:1, :block_len])], 0
    )
    value_out = value_grad[:, block_len:] + jnp.concatenate(
        [value_grad[1:, :block_len], jnp.zeros_like(value_grad[:1, :block_len])], 0
    )
    return (key_out, value_out)


def attend_heads(q_tiles, kv_tiles, do_tiles, stat_tiles, fill_tiles, cont_tiles):
    tile_total, block_len = (q_tiles.shape[0], q_tiles.shape[1])
    kv_cols = kv_tiles.shape[3]
    kv_local = kv_cols // HD
    group_size = q_tiles.shape[2] // kv_cols
    q_heads = q_tiles.reshape(tile_total, block_len, kv_local, group_size, HD)
    do_heads = do_tiles.reshape(tile_total, block_len, kv_local, group_size, HD)
    stat_heads = stat_tiles.reshape(tile_total, block_len, 2, kv_local, group_size)
    results = []
    for head_index in range(kv_local):
        low_col = head_index * HD
        key_out, value_out = band_grads(
            q_heads[:, :, head_index],
            kv_tiles[:, :, 0, low_col : low_col + HD],
            kv_tiles[:, :, 1, low_col : low_col + HD],
            do_heads[:, :, head_index],
            stat_heads[:, :, 0, head_index],
            stat_heads[:, :, 1, head_index],
            fill_tiles,
            cont_tiles,
        )
        results.append(jnp.stack([key_out, value_out], 2))
    return jnp.concatenate(results, 3).astype(jnp.bfloat16)


def per_device(
    layer_input,
    queries,
    keys_values,
    out_grads,
    log_sums,
    deltas,
    tile_fill,
    tile_cont,
    moment_first,
    moment_second,
):
    group_count = lax.axis_size("dp")
    tile_count = tile_fill.shape[1]
    token_count = queries.shape[0]
    block_len = token_count // tile_count
    my_group = lax.axis_index("dp")
    q_tiles = queries.reshape(tile_count, block_len, -1)
    kv_tiles = keys_values.reshape(tile_count, block_len, 2, -1)
    do_tiles = out_grads.reshape(tile_count, block_len, -1)
    stat_tiles = jnp.stack([log_sums, deltas], 1).reshape(tile_count, block_len, 2, -1)
    fill_mine = lax.dynamic_index_in_dim(tile_fill, my_group, 0, keepdims=False)
    cont_mine = lax.dynamic_index_in_dim(tile_cont, my_group, 0, keepdims=False)
    kv_grads = attend_heads(q_tiles, kv_tiles, do_tiles, stat_tiles, fill_mine, cont_mine)
    kv_grads = kv_grads.reshape(token_count, 2, -1)
    terms = jnp.einsum(
        "tr,tkc->rkc",
        layer_input,
        lax.all_gather(kv_grads, "tensor", axis=2, tiled=True),
        preferred_element_type=jnp.float32,
    )
    summed = lax.psum_scatter(terms, "dp", scatter_dimension=0, tiled=True)
    proj_grads = summed / math.sqrt(token_count * group_count)
    new_first = ADAM_ONE * moment_first + (1 - ADAM_ONE) * proj_grads
    heads_kv = moment_second.shape[1]
    partial_squares = jnp.sum(
        jnp.square(proj_grads).reshape(proj_grads.shape[0], 2, heads_kv, -1), axis=(0, 3)
    )
    squares = lax.psum(partial_squares, ("dp", "tensor"))
    new_second = ADAM_TWO * moment_second + (1 - ADAM_TWO) * squares / (D * HD)
    step_size = jnp.sqrt(new_second / (1 - ADAM_TWO**2)) + ADAM_EPS
    scaled = (new_first / (1 - ADAM_ONE**2)).reshape(proj_grads.shape[0], 2, heads_kv, -1)
    update = (scaled / step_size[None, :, :, None]).reshape(proj_grads.shape)
    return (update, new_first, new_second)


def solution(mesh):
    in_specs = (
        P("dp", "tensor"),
        P("dp", "tensor"),
        P("dp", None, "tensor"),
        P("dp", "tensor"),
        P("dp", "tensor"),
        P("dp", "tensor"),
        P(),
        P(),
        P(("tensor", "dp"), None, None),
        P(),
    )
    out_specs = (P(("tensor", "dp"), None, None), P(("tensor", "dp"), None, None), P())
    return jax.shard_map(
        per_device, mesh=mesh, in_specs=in_specs, out_specs=out_specs, check_vma=False
    )
```

profile of v0, /device:TPU:0, one launch (start us, length us, event | category | flops | bytes accessed | tf_op | source)
XLA Modules:
  0.0 350.4 jit_solution(9090283319070825680)
XLA Ops:
  7.3 1.9 copy.44
  9.1 1.7 slice_bitcast_fusion.2
  10.8 1.7 slice_bitcast_fusion.6
  12.5 0.7 compare_bitcast_fusion
  13.3 2.6 reshape.151
  15.8 4.0 %reshape.152 = bf16[16,128,2,2,128]{4,3,2,1,0:T(2,128)(2,1)} reshape(bf16[2048,512]{1,0:T(8,128)(2,1)} %param.13) | data formatting | bytes 4194304 | tf_op jit(solution)/shard_map/reshape;reshape | solution.py:67
  20.2 6.1 %fusion.107 = (bf16[16,128,1,2,128]{4,3,2,1,0:T(2,128)(2,1)S(1)}, bf16[16,128,1,2,128]{4,3,2,1,0:T(2,128)(2,1)}, bf16[16,128,1,2,128]{4,3,2,1,0:T(2,128)(2,1)S(1)}, bf16[16,128,1,2,128]{4,3,2,1,0:T(2,128)(2,1)S(1)}) fusion(bf16[16,128,2,2,128]{4,3,2,1,0:T(2,128)(2,1)} %reshape.152, bf16[16,128,2,2,128]{4,3,2,1,0:T(2,128)(2,1)S(1)} %reshape.151), kind=kLoop, calls=%fused_computation.126 | loop fusion | bytes 8388608 | tf_op jit(solution)/shard_map/slice | solution.py:76
  26.4 0.9 copy-done.4
  27.3 0.7 fusion.39
  28.1 2.5 fusion.31
  31.1 6.2 %bitcast_multiply_fusion.1 = f32[16,256,128]{2,1,0:T(8,128)} fusion(f32[16,256,128,2]{2,1,3,0:T(8,128)} %copy-done.3, f32[16,2,128]{2,1,0:T(2,128)S(1)} %get-tuple-element.37, f32[16,2,128]{2,1,0:T(2,128)S(1)} %get-tuple-element.35, pred[16,128,256]{1,2,0:T(8,128)(4,1)} %copy-done.14, bf16[15,128,128]{2,1,0:T(8,128)(2,1)S(1)} %copy-done.18, ...), kind=kOutput, calls=%fused_computation.26 | convolution fusion | flops 546832384 | bytes 9961472 | tf_op jit(solution)/shard_map/sgqk,sqgd->skd/dot_general | solution.py:44
  37.3 1.4 slice.129
  38.6 1.4 fusion.59
  40.3 0.7 fusion.47
  41.6 2.5 fusion.34
  44.2 6.1 %bitcast_multiply_fusion = f32[16,256,128]{2,1,0:T(8,128)} fusion(f32[16,256,128,2]{2,1,3,0:T(8,128)} %copy-done.2, f32[16,2,128]{2,1,0:T(2,128)S(1)} %get-tuple-element.36, f32[16,2,128]{2,1,0:T(2,128)S(1)} %get-tuple-element.34, pred[16,128,256]{1,2,0:T(8,128)(4,1)S(1)} %copy-done.16, bf16[15,128,128]{2,1,0:T(8,128)(2,1)} %get-tuple-element.21, ...), kind=kOutput, calls=%fused_computation.25 | convolution fusion | flops 546832384 | bytes 9961472 | tf_op jit(solution)/shard_map/sgqk,sqgd->skd/dot_general | solution.py:44
  50.2 1.3 slice.141
  51.5 1.4 fusion.54
  53.2 1.3 slice.131
  54.5 1.4 fusion.58
  56.1 1.3 slice.143
  57.4 1.4 fusion.53
  59.0 1.5 maximum_maximum_fusion
  60.7 152.4 %all-gather.2.cloned.1.call-done = bf16[2048,2,1024]{0,2,1:T(8,128)(2,1)} async-done(((bf16[2048,2,256]{0,2,1:T(8,128)(2,1)}), bf16[2048,2,1024]{0,2,1:T(8,128)(2,1)}) %all-gather.2.cloned.1.call-update) | async-done | bytes 8388624 | tf_op jit(solution)/shard_map/all_gather | solution.py:114
  213.1 14.4 %fusion.10 = f32[1024,2,1024]{0,2,1:T(8,128)} fusion(bf16[2048,2,1024]{0,2,1:T(8,128)(2,1)} %all-gather.2.cloned.1.call-done, bf16[2048,1024]{1,0:T(8,128)(2,1)} %param.10), kind=kOutput, calls=%fused_computation.14 | convolution fusion | flops 8589934592 | bytes 20971520 | tf_op jit(solution)/shard_map/tr,tkc->rkc/dot_general | solution.py:111
  227.5 69.6 %reduce-scatter.2.cloned.1.call-done = f32[128,2,1024]{0,2,1:T(8,128)} async-done(((f32[1024,2,1024]{0,2,1:T(8,128)}), f32[128,2,1024]{0,2,1:T(8,128)}) %reduce-scatter.2.cloned.1.call-update) | async-done | bytes 1048592 | tf_op jit(solution)/shard_map/reduce_scatter | solution.py:117
  297.1 1.6 multiply_reduce_fusion
  299.3 39.3 %psum.7 = f32[2,8]{1,0:T(2,128)S(1)} all-reduce(f32[2,8]{1,0:T(2,128)S(1)} %bitcast_reduce_fusion), channel_id=1, replica_groups=mesh['dp'=8,'tensor'=4] {'dp','tensor'}, use_global_device_ids=true, to_apply=%region_3.4 | all-reduce | flops 16 | bytes 128 | tf_op jit(solution)/shard_map/psum | solution.py:124
  338.6 0.6 sqrt_add_fusion
  339.3 1.6 multiply_divide_fusion
  340.9 1.3 copy.59
  342.2 1.3 copy.60
  (67 shorter events, 3.3 us)
Async XLA Ops:
  7.2 6.1 %copy-start = (s32[8,16]{1,0:T(8,128)S(1)}, s32[8,16]{1,0:T(8,128)}, u32[]{:S(2)}) copy-start(s32[8,16]{1,0:T(8,128)} %param.16) | copy-start | bytes 1540
  7.2 205.9 %all-gather.2.cloned.1.call-start = ((), (), s32[]{:S(2)}) async-start(), calls=%async_computation.1 | async-start | bytes 10485760 | tf_op jit(solution)/shard_map/all_gather | solution.py:114
  13.2 6.6 %copy-start.19 = (bf16[2048,4]{0,1:T(4,128)(2,1)S(1)}, bf16[2048,4]{0,1:T(4,128)(2,1)}, u32[]{:S(2)}) copy-start(bf16[2048,4]{0,1:T(4,128)(2,1)} %param.14) | copy-start | bytes 49156
  13.2 6.6 %copy-start.20 = (bf16[2048,4]{0,1:T(4,128)(2,1)S(1)}, bf16[2048,4]{0,1:T(4,128)(2,1)}, u32[]{:S(2)}) copy-start(bf16[2048,4]{0,1:T(4,128)(2,1)} %param.15) | copy-start | bytes 49156
  20.2 7.9 %copy-start.14 = (pred[16,128,256]{1,2,0:T(8,128)(4,1)}, pred[16,128,256]{1,2,0:T(8,128)(4,1)S(1)}, u32[]{:S(2)}) copy-start(pred[16,128,256]{1,2,0:T(8,128)(4,1)S(1)} %pad_add_fusion) | copy-start | bytes 1572868
  20.2 7.1 %copy-start.7 = (bf16[16,128,128]{2,1,0:T(8,128)(2,1)S(1)}, bf16[16,128,128]{2,1,0:T(8,128)(2,1)}, u32[]{:S(2)}) copy-start(bf16[16,128,128]{2,1,0:T(8,128)(2,1)} %get-tuple-element.19) | copy-start | bytes 1572868
  20.2 7.1 %copy-start.9 = (bf16[15,128,128]{2,1,0:T(8,128)(2,1)S(1)}, bf16[15,128,128]{2,1,0:T(8,128)(2,1)}, u32[]{:S(2)}) copy-start(bf16[15,128,128]{2,1,0:T(8,128)(2,1)} %get-tuple-element.23) | copy-start | bytes 1474564
  26.4 1.0 copy-start.4
  26.4 4.2 %copy-start.13 = (bf16[16,128,1,2,128]{4,3,2,1,0:T(2,128)(2,1)}, bf16[16,128,1,2,128]{4,3,2,1,0:T(2,128)(2,1)S(1)}, u32[]{:S(2)}) copy-start(bf16[16,128,1,2,128]{4,3,2,1,0:T(2,128)(2,1)S(1)} %get-tuple-element.24) | copy-start | bytes 3145732
  28.0 2.8 copy-start.3
  28.1 2.8 copy-start.5
  28.1 2.8 copy-start.17
  28.1 3.0 copy-start.18
  37.3 3.0 copy-start.6
  37.3 3.1 copy-start.8
  40.3 1.2 copy-start.11
  40.3 1.3 copy-start.15
  41.0 3.1 copy-start.2
  41.6 2.5 copy-start.12
  41.6 2.5 copy-start.16
  60.6 236.5 %reduce-scatter.2.cloned.1.call-start = ((), (), s32[]{:S(2)}) async-start(), calls=%async_computation.2 | async-start | bytes 9437184 | tf_op jit(solution)/shard_map/reduce_scatter | solution.py:117
  227.5 71.3 %copy-start.10 = (f32[128,2,1024]{2,1,0:T(2,128)S(1)}, f32[128,2,1024]{2,1,0:T(2,128)}, u32[]{:S(2)}) copy-start(f32[128,2,1024]{2,1,0:T(2,128)} %param.18) | copy-start | bytes 3145732
  227.5 111.1 %copy-start.21 = (f32[2,8]{1,0:T(2,128)S(1)}, f32[2,8]{1,0:T(2,128)}, u32[]{:S(2)}) copy-start(f32[2,8]{1,0:T(2,128)} %param.19) | copy-start | bytes 196
  339.3 4.2 %copy-start.1 = (s32[8,16]{1,0:T(8,128)S(1)}, s32[8,16]{1,0:T(8,128)}, u32[]{:S(2)}) copy-start(s32[8,16]{1,0:T(8,128)} %param.16) | copy-start | bytes 1540
Sparse Core Ops, SparseCore 0:
  60.7 152.3 all-gather.1
  227.6 69.4 reduce-scatter.1
where the time goes:
time: 351 us; the launch traced here: 350 us
  waiting for transfers between devices  222 us (63%)
  blocking collectives  39.3 us (11%)
  matrix products  33 us (9%)
  local copies, waits for them, and re-layouts  29.4 us (8%)
  between operations  14.4 us (4%)
  other arithmetic  12.1 us (3%)
    all_gather x1, waiting for transfers between devices, per_device(): lax.all_gather(kv_grads, 'tensor', axis=2, tiled=True)  152 us
    reduce_scatter x1, waiting for transfers between devices, per_device(): summed = lax.psum_scatter(terms, 'dp', scatter_dimension=0, tiled=True)  69.6 us
    psum x1, blocking collectives, per_device(): squares = lax.psum(partial_squares, ('dp', 'tensor'))  39.3 us
    dot_general x1, matrix products, per_device(): jnp.einsum('tr,tkc->rkc', layer_input, lax.all_gather(kv_grads, 'tensor',...  14.4 us
    dot_general x2, matrix products, band_grads(): jnp.einsum('sgqk,sqgd->skd', dscores.astype(jnp.bfloat16), q_tiles, prefe...  12.3 us
    unnamed x52, local copies, waits for them, and re-layouts  7.17 us
  transfers between devices with their start and end apart: 2, of which 2 were waited for; matrix products, arithmetic and copies ran while one was open for 0% of the time, Pallas kernels for 0%

commit v1 on v0

--- a/solution.py
+++ b/solution.py
@@ -9,6 +9,18 @@
 ADAM_ONE = 0.9
 ADAM_TWO = 0.95
 ADAM_EPS = 1e-08
+
+
+def collect(array, axis, dim):
+    ways, here, step = (lax.axis_size(axis), lax.axis_index(axis), array.shape[dim])
+    line, have = (array, 1)
+    while have < ways:
+        line = jnp.concatenate(
+            [line, lax.ppermute(line, axis, [(d, (d - have) % ways) for d in range(ways)])],
+            axis=dim,
+        )
+        have = 2 * have
+    return jnp.roll(line, here * step, axis=dim)
 
 
 def band_grads(q_tiles, k_tiles, v_tiles, do_tiles, lse_tiles, delta_tiles, fill_tiles, cont_tiles):
@@ -111,7 +123,7 @@
     terms = jnp.einsum(
         "tr,tkc->rkc",
         layer_input,
-        lax.all_gather(kv_grads, "tensor", axis=2, tiled=True),
+        collect(kv_grads, "tensor", 2),
         preferred_element_type=jnp.float32,
     )
     summed = lax.psum_scatter(terms, "dp", scatter_dimension=0, tiled=True)

time: 351 us -> 441 us (1.26)
  waiting for transfers between devices: 222 us -> 295 us
  local copies, waits for them, and re-layouts: 29.4 us -> 36.7 us
  starting transfers between devices: 0.08 us -> 6.63 us
  other arithmetic: 12.1 us -> 17.1 us
    ppermute x0 -> x2, waiting for transfers between devices: none -> 224 us  [collect(): lax.ppermute(line, axis, [(d, (d - have) % ways) for d in range(ways)])]
    all_gather x1 -> x0, waiting for transfers between devices: 152 us -> none  [per_device(): lax.all_gather(kv_grads, 'tensor', axis=2, tiled=True)]
    ppermute x0 -> x2, starting transfers between devices: none -> 6.59 us  [collect(): lax.ppermute(line, axis, [(d, (d - have) % ways) for d in range(ways)])]
    unnamed x52 -> x59, local copies, waits for them, and re-layouts: 7.17 us -> 10.6 us
  transfers between devices with their start and end apart: 2 -> 3, of which waited for: 2 -> 3; matrix products, arithmetic and copies ran while one was open for 0% -> 1% of each run, Pallas kernels for 0% -> 0%
where the time goes in v1:
time: 441 us; the launch traced here: 440 us
  waiting for transfers between devices  295 us (67%)
  blocking collectives  39.3 us (9%)
  local copies, waits for them, and re-layouts  36.7 us (8%)
  matrix products  30.7 us (7%)
  other arithmetic  17.1 us (4%)
  between operations  14.5 us (3%)
  starting transfers between devices  6.63 us (2%)
    ppermute x2, waiting for transfers between devices, collect(): lax.ppermute(line, axis, [(d, (d - have) % ways) for d in range(ways)])  224 us
    reduce_scatter x1, waiting for transfers between devices, per_device(): summed = lax.psum_scatter(terms, 'dp', scatter_dimension=0, tiled=True)  71.5 us
    psum x1, blocking collectives, per_device(): squares = lax.psum(partial_squares, ('dp', 'tensor'))  39.3 us
    dot_general x2, matrix products, band_grads(): jnp.einsum('sgqk,sqgd->skd', dscores.astype(jnp.bfloat16), q_tiles, prefe...  12.1 us
    dot_general x1, matrix products, per_device(): jnp.einsum('tr,tkc->rkc', layer_input, collect(kv_grads, 'tensor', 2), pr...  11 us
    unnamed x59, local copies, waits for them, and re-layouts  10.6 us
  transfers between devices with their start and end apart: 3, of which 3 were waited for; matrix products, arithmetic and copies ran while one was open for 1% of the time, Pallas kernels for 0%

profile of v1, /device:TPU:0, one launch (start us, length us, event | category | flops | bytes accessed | tf_op | source)
XLA Modules:
  0.0 440.0 jit_solution(1646832624500487148)
XLA Ops:
  7.3 1.9 copy.44
  9.1 1.7 slice_bitcast_fusion
  10.9 1.6 slice_bitcast_fusion.4
  13.2 2.6 reshape.151
  15.8 4.0 reshape.152
  20.2 7.1 %fusion.116 = (bf16[16,128,1,2,128]{4,3,2,1,0:T(2,128)(2,1)S(1)}, bf16[16,128,1,2,128]{4,3,2,1,0:T(2,128)(2,1)}, bf16[16,128,1,2,128]{4,3,2,1,0:T(2,128)(2,1)}, bf16[16,128,1,2,128]{4,3,2,1,0:T(2,128)(2,1)S(1)}) fusion(bf16[16,128,2,2,128]{4,3,2,1,0:T(2,128)(2,1)} %reshape.152, bf16[16,128,2,2,128]{4,3,2,1,0:T(2,128)(2,1)S(1)} %reshape.151), kind=kLoop, calls=%fused_computation.141 | loop fusion | bytes 8388608 | tf_op jit(solution)/shard_map/slice | solution.py:88
  28.1 2.6 fusion.37
  30.7 6.1 %bitcast_multiply_fusion = f32[16,256,128]{2,1,0:T(8,128)} fusion(f32[16,256,128,2]{2,1,3,0:T(8,128)} %copy-done.7, f32[16,2,128]{2,1,0:T(2,128)S(1)} %get-tuple-element.36, f32[16,2,128]{2,1,0:T(2,128)S(1)} %get-tuple-element.34, pred[16,128,256]{1,2,0:T(8,128)(4,1)} %copy-done.16, bf16[15,128,128]{2,1,0:T(8,128)(2,1)S(1)} %copy-done.19, ...), kind=kOutput, calls=%fused_computation.27 | convolution fusion | flops 546832384 | bytes 9961472 | tf_op jit(solution)/shard_map/sgqk,sqgd->skd/dot_general | solution.py:56
  36.8 1.4 slice.141
  38.2 1.4 fusion.57
  39.9 1.8 fusion.42
  41.7 2.4 fusion.34
  44.3 6.0 %bitcast_multiply_fusion.1 = f32[16,256,128]{2,1,0:T(8,128)} fusion(f32[16,256,128,2]{2,1,3,0:T(8,128)} %copy-done.6, f32[16,2,128]{2,1,0:T(2,128)S(1)} %get-tuple-element.37, f32[16,2,128]{2,1,0:T(2,128)S(1)} %get-tuple-element.35, pred[16,128,256]{1,2,0:T(8,128)(4,1)S(1)} %copy-done.17, bf16[15,128,128]{2,1,0:T(8,128)(2,1)} %get-tuple-element.22, ...), kind=kOutput, calls=%fused_computation.28 | convolution fusion | flops 546832384 | bytes 9961472 | tf_op jit(solution)/shard_map/sgqk,sqgd->skd/dot_general | solution.py:56
  51.6 1.3 fusion.62
  53.1 1.3 slice.143
  54.4 1.3 fusion.56
  56.0 1.5 slice.131
  57.4 1.3 fusion.61
  60.0 5.1 %collective-permute-start = (bf16[2048,2,256]{0,2,1:T(8,128)(2,1)S(1)}, bf16[2048,2,256]{0,2,1:T(8,128)(2,1)S(1)}, u32[]{:S(2)}, u32[]{:S(2)}) collective-permute-start(bf16[2048,2,256]{0,2,1:T(8,128)(2,1)S(1)} %maximum_maximum_fusion), channel_id=1, source_target_pairs={{0,3},{1,0},{2,1},{3,2},{4,7},{5,4},{6,5},{7,6},{8,11},{9,8},{10,9... | collective-permute-start | bytes 6291464 | tf_op jit(solution)/shard_map/ppermute | solution.py:19
  65.1 44.9 %collective-permute-done = bf16[2048,2,256]{0,2,1:T(8,128)(2,1)S(1)} collective-permute-done((bf16[2048,2,256]{0,2,1:T(8,128)(2,1)S(1)}, bf16[2048,2,256]{0,2,1:T(8,128)(2,1)S(1)}, u32[]{:S(2)}, u32[]{:S(2)}) %collective-permute-start) | collective-permute-done | bytes 2097184 | tf_op jit(solution)/shard_map/ppermute | solution.py:19
  110.0 3.3 pad_maximum_fusion
  113.3 1.5 collective-permute-start.1
  117.3 178.6 %collective-permute-done.1 = bf16[2048,2,512]{0,2,1:T(8,128)(2,1)} collective-permute-done((bf16[2048,2,512]{0,2,1:T(8,128)(2,1)}, bf16[2048,2,512]{0,2,1:T(8,128)(2,1)}, u32[]{:S(2)}, u32[]{:S(2)}) %collective-permute-start.1) | collective-permute-done | bytes 4194336 | tf_op jit(solution)/shard_map/ppermute | solution.py:19
  295.9 2.7 constant_dynamic-update-slice_fusion.2
  299.0 2.9 constant_dynamic-update-slice_fusion
  302.4 11.0 %fusion.11 = f32[1024,2,1024]{0,2,1:T(8,128)} fusion(bf16[2048,1024]{1,0:T(8,128)(2,1)S(1)} %copy-done.23, bf16[2048,2,2048]{0,2,1:T(8,128)(2,1)S(1)} %constant_dynamic-update-slice_fusion, s32[]{:T(128)S(6)} %select_n.29), kind=kOutput, calls=%fused_computation.16 | convolution fusion | flops 8589934592 | bytes 20971524 | tf_op jit(solution)/shard_map/tr,tkc->rkc/dot_general | solution.py:123
  313.4 71.5 %reduce-scatter.2.cloned.1.call-done = f32[128,2,1024]{0,2,1:T(8,128)} async-done(((f32[1024,2,1024]{0,2,1:T(8,128)}), f32[128,2,1024]{0,2,1:T(8,128)}) %reduce-scatter.2.cloned.1.call-update) | async-done | bytes 1048592 | tf_op jit(solution)/shard_map/reduce_scatter | solution.py:129
  384.9 1.6 multiply_reduce_fusion
  387.1 39.3 %psum.7 = f32[2,8]{1,0:T(2,128)S(1)} all-reduce(f32[2,8]{1,0:T(2,128)S(1)} %bitcast_reduce_fusion), channel_id=1, replica_groups=mesh['dp'=8,'tensor'=4] {'dp','tensor'}, use_global_device_ids=true, to_apply=%region_3.4 | all-reduce | flops 16 | bytes 128 | tf_op jit(solution)/shard_map/psum | solution.py:136
  427.0 2.6 multiply_divide_fusion
  429.6 2.3 copy.59
  431.8 1.3 copy.60
  (81 shorter events, 9.7 us)
Async XLA Ops:
  7.2 6.0 %copy-start = (s32[8,16]{1,0:T(8,128)S(1)}, s32[8,16]{1,0:T(8,128)}, u32[]{:S(2)}) copy-start(s32[8,16]{1,0:T(8,128)} %param.16) | copy-start | bytes 1540
  7.2 377.7 %reduce-scatter.2.cloned.1.call-start = ((), (), s32[]{:S(2)}) async-start(), calls=%async_computation.1 | async-start | bytes 9437184 | tf_op jit(solution)/shard_map/reduce_scatter | solution.py:129
  13.2 6.6 %copy-start.20 = (bf16[2048,4]{0,1:T(4,128)(2,1)S(1)}, bf16[2048,4]{0,1:T(4,128)(2,1)}, u32[]{:S(2)}) copy-start(bf16[2048,4]{0,1:T(4,128)(2,1)} %param.14) | copy-start | bytes 49156
  13.2 6.6 %copy-start.21 = (bf16[2048,4]{0,1:T(4,128)(2,1)S(1)}, bf16[2048,4]{0,1:T(4,128)(2,1)}, u32[]{:S(2)}) copy-start(bf16[2048,4]{0,1:T(4,128)(2,1)} %param.15) | copy-start | bytes 49156
  20.2 7.9 %copy-start.16 = (pred[16,128,256]{1,2,0:T(8,128)(4,1)}, pred[16,128,256]{1,2,0:T(8,128)(4,1)S(1)}, u32[]{:S(2)}) copy-start(pred[16,128,256]{1,2,0:T(8,128)(4,1)S(1)} %pad_add_fusion) | copy-start | bytes 1572868
  20.2 7.1 %copy-start.10 = (bf16[16,128,128]{2,1,0:T(8,128)(2,1)S(1)}, bf16[16,128,128]{2,1,0:T(8,128)(2,1)}, u32[]{:S(2)}) copy-start(bf16[16,128,128]{2,1,0:T(8,128)(2,1)} %get-tuple-element.17) | copy-start | bytes 1572868
  20.2 7.1 %copy-start.11 = (bf16[15,128,128]{2,1,0:T(8,128)(2,1)S(1)}, bf16[15,128,128]{2,1,0:T(8,128)(2,1)}, u32[]{:S(2)}) copy-start(bf16[15,128,128]{2,1,0:T(8,128)(2,1)} %get-tuple-element.21) | copy-start | bytes 1474564
  27.3 3.4 copy-start.15
  28.1 2.7 copy-start.7
  28.1 2.6 copy-start.18
  28.1 2.6 copy-start.19
  36.8 3.0 copy-start.8
  36.8 3.0 copy-start.9
  39.6 2.1 copy-start.17
  39.8 1.9 copy-start.13
  41.7 2.6 copy-start.6
  41.7 2.6 copy-start.14
  56.0 3.0 copy-start.2
  59.0 0.8 copy-start.4
  60.0 50.0 %collective-permute-start = (bf16[2048,2,256]{0,2,1:T(8,128)(2,1)S(1)}, bf16[2048,2,256]{0,2,1:T(8,128)(2,1)S(1)}, u32[]{:S(2)}, u32[]{:S(2)}) collective-permute-start(bf16[2048,2,256]{0,2,1:T(8,128)(2,1)S(1)} %maximum_maximum_fusion), channel_id=1, source_target_pairs={{0,3},{1,0},{2,1},{3,2},{4,7},{5,4},{6,5},{7,6},{8,11},{9,8},{10,9... | collective-permute-start | bytes 6291464 | tf_op jit(solution)/shard_map/ppermute | solution.py:19
  113.3 182.6 %collective-permute-start.1 = (bf16[2048,2,512]{0,2,1:T(8,128)(2,1)}, bf16[2048,2,512]{0,2,1:T(8,128)(2,1)}, u32[]{:S(2)}, u32[]{:S(2)}) collective-permute-start(bf16[2048,2,512]{0,2,1:T(8,128)(2,1)} %pad_maximum_fusion), channel_id=1, source_target_pairs={{0,2},{1,3},{2,0},{3,1},{4,6},{5,7},{6,4},{7,5},{8,10},{9,11},{10,... | collective-permute-start | bytes 12582920 | tf_op jit(solution)/shard_map/ppermute | solution.py:19
  117.2 181.4 %copy-start.5 = (bf16[2048,1,128]{0,2,1:T(8,128)(2,1)S(1)}, bf16[2048,1,128]{0,2,1:T(8,128)(2,1)}, u32[]{:S(2)}) copy-start(bf16[2048,1,128]{0,2,1:T(8,128)(2,1)} %copy-done.4) | copy-start | bytes 1572868
  117.2 181.4 %copy-start.3 = (bf16[2048,1,128]{0,2,1:T(8,128)(2,1)S(1)}, bf16[2048,1,128]{0,2,1:T(8,128)(2,1)}, u32[]{:S(2)}) copy-start(bf16[2048,1,128]{0,2,1:T(8,128)(2,1)} %copy-done.2) | copy-start | bytes 1572868
  298.9 3.5 copy-start.23
  313.4 73.1 %copy-start.12 = (f32[128,2,1024]{2,1,0:T(2,128)S(1)}, f32[128,2,1024]{2,1,0:T(2,128)}, u32[]{:S(2)}) copy-start(f32[128,2,1024]{2,1,0:T(2,128)} %param.18) | copy-start | bytes 3145732
  313.4 113.0 %copy-start.22 = (f32[2,8]{1,0:T(2,128)S(1)}, f32[2,8]{1,0:T(2,128)}, u32[]{:S(2)}) copy-start(f32[2,8]{1,0:T(2,128)} %param.19) | copy-start | bytes 196
  427.0 6.1 %copy-start.1 = (s32[8,16]{1,0:T(8,128)S(1)}, s32[8,16]{1,0:T(8,128)}, u32[]{:S(2)}) copy-start(s32[8,16]{1,0:T(8,128)} %param.16) | copy-start | bytes 1540
Sparse Core Ops, SparseCore 0:
  313.6 71.2 reduce-scatter.1
